TPU v7x, 32 devices: a whole 2x2x4 slice. The times are simulated.
32 devices in a mesh: dp: 8 (over z, x), txt: 4 (over y, core).
Axes of the slice: x: 2, y: 2, z: 4, core: 2. Of those that a mesh axis runs over, the one named last changes fastest.
Arguments:
- resid: bfloat16 [2048, 1024], P('dp', 'txt'), may hold values from -40 to 40
- prenorm_gain: float32 [1024], replicated, may hold values from 0.25 to 1.75
- prenorm_bias: float32 [1024], replicated, may hold values from -3 to 3
- up_weight: bfloat16 [1024, 4096], P('dp', 'txt'), may hold values from -0.1875 to 0.1875
- up_bias: float32 [4096], P('txt'), may hold values from -3 to 3
- down_weight: bfloat16 [4096, 1024], P('txt', 'dp'), may hold values from -0.09375 to 0.09375
- down_bias: float32 [1024], replicated, may hold values from -3 to 3
- post_gain: float32 [1024], P('txt'), may hold values from 0.25 to 1.75
- post_bias: float32 [1024], P('txt'), may hold values from -3 to 3
- projection: bfloat16 [1024, 768], P('txt'), may hold values from -1 to 1
- texts: bfloat16 [5120, 768], P('txt'), may hold values from -48 to 48
- labels: int32 [2048], P('dp'), may hold values from 0 to 5119
- step_size: float32 [1], replicated, may hold values from 0.5 to 2
Outputs:
- adversarial: float32 [2048, 1024], P('dp', 'txt')
All inputs are finite; a program needn't handle non-finite values.
Results may differ from a plain program's by a relative error of at most 0.0036.
Values may be sent and summed in bfloat16 or wider, within the bound.
A program may use at most 64 MiB of HBM per device.

v0:
```python
import jax
import jax.numpy as jnp
from jax import lax
from jax.sharding import PartitionSpec as P

MODEL_WIDTH = 1024


def local(
    resid,
    prenorm_gain,
    prenorm_bias,
    up_weight,
    up_bias,
    down_weight,
    down_bias,
    post_gain,
    post_bias,
    projection,
    texts,
    labels,
    step_size,
):
    feature_width = resid.shape[1]
    shift_amount = lax.axis_index("txt") * feature_width
    gathered = lax.all_gather(resid, "txt", axis=1, tiled=True)
    input_rows = gathered.astype(jnp.float32)
    input_mean = jnp.mean(input_rows, axis=1, keepdims=True)
    var_in = jnp.mean(input_rows * input_rows, axis=1, keepdims=True) - input_mean * input_mean
    input_inverse_deviation = lax.rsqrt(var_in + 1e-05)
    centered_input = (input_rows - input_mean) * input_inverse_deviation
    normed_input = (centered_input * prenorm_gain + prenorm_bias).astype(jnp.bfloat16)
    w_up = lax.all_gather(up_weight, "dp", axis=0, tiled=True)
    w_down = lax.all_gather(down_weight, "dp", axis=1, tiled=True)
    pre_act = jnp.dot(normed_input, w_up, preferred_element_type=jnp.float32) + up_bias
    gate_sig = jax.nn.sigmoid(1.702 * pre_act)
    hidden = (pre_act * gate_sig).astype(jnp.bfloat16)
    mixed_part = jnp.dot(hidden, w_down, preferred_element_type=jnp.float32)
    mixed = lax.psum_scatter(mixed_part, "txt", scatter_dimension=1, tiled=True)
    own_rows = resid.astype(jnp.float32)
    block_out = own_rows + mixed + lax.dynamic_slice_in_dim(down_bias, shift_amount, feature_width)
    out_sums = lax.psum((jnp.sum(block_out, axis=1), jnp.sum(block_out * block_out, axis=1)), "txt")
    mean_out = out_sums[0][:, None] / MODEL_WIDTH
    var_out = out_sums[1][:, None] / MODEL_WIDTH - mean_out * mean_out
    rstd_out = lax.rsqrt(var_out + 1e-05)
    yhat = (block_out - mean_out) * rstd_out
    post_normed = (yhat * post_gain + post_bias).astype(jnp.bfloat16)
    emb_part = jnp.dot(post_normed, projection, preferred_element_type=jnp.float32)
    embedding = lax.psum_scatter(emb_part, "txt", scatter_dimension=0, tiled=True)
    emb_norm = jnp.sqrt(jnp.sum(embedding * embedding, axis=1, keepdims=True) + 1e-06)
    unit_vec = embedding / emb_norm
    unit_low = lax.all_gather(unit_vec.astype(jnp.bfloat16), "txt", axis=0, tiled=True)
    text_f = texts.astype(jnp.float32)
    text_unit = (text_f / jnp.sqrt(jnp.sum(text_f * text_f, axis=1, keepdims=True) + 1e-06)).astype(
        jnp.bfloat16
    )
    logits = 100.0 * jnp.einsum(
        "ie,je->ij", unit_low, text_unit, preferred_element_type=jnp.float32
    )
    local_top = jnp.max(logits, axis=1)
    row_top = lax.pmax(local_top, "txt")
    exponent = jnp.exp(logits - row_top[:, None])
    row_total = lax.psum(jnp.sum(exponent, axis=1), "txt")
    prob = exponent / row_total[:, None]
    local_label = labels - lax.axis_index("txt") * texts.shape[0]
    columns = lax.broadcasted_iota(jnp.int32, logits.shape, 1)
    target = (columns == local_label[:, None]).astype(jnp.float32)
    score_grad = (100.0 * (prob - target)).astype(jnp.bfloat16)
    back_part = jnp.dot(score_grad, text_unit, preferred_element_type=jnp.float32)
    unit_grad = lax.psum_scatter(back_part, "txt", scatter_dimension=0, tiled=True)
    along = jnp.sum(unit_vec * unit_grad, axis=1, keepdims=True)
    grad_share = ((unit_grad - unit_vec * along) / emb_norm).astype(jnp.bfloat16)
    emb_grad = lax.all_gather(grad_share, "txt", axis=0, tiled=True)
    post_grad = jnp.einsum("ie,de->id", emb_grad, projection, preferred_element_type=jnp.float32)
    scaled = post_grad * post_gain
    back_sums = lax.psum((jnp.sum(scaled, axis=1), jnp.sum(scaled * yhat, axis=1)), "txt")
    output_gradient = (
        scaled - back_sums[0][:, None] / MODEL_WIDTH - yhat * (back_sums[1][:, None] / MODEL_WIDTH)
    ) * rstd_out
    out_full = lax.all_gather(output_gradient.astype(jnp.bfloat16), "txt", axis=1, tiled=True)
    hid_grad = jnp.einsum("id,fd->if", out_full, w_down, preferred_element_type=jnp.float32)
    act_grad = (hid_grad * (gate_sig + 1.702 * pre_act * gate_sig * (1.0 - gate_sig))).astype(
        jnp.bfloat16
    )
    normed_part = jnp.einsum("if,df->id", act_grad, w_up, preferred_element_type=jnp.float32)
    normed_gradient = lax.psum_scatter(normed_part, "txt", scatter_dimension=1, tiled=True)
    centered_input_portion = lax.dynamic_slice_in_dim(
        centered_input, shift_amount, feature_width, 1
    )
    scaled_input = normed_gradient * lax.dynamic_slice_in_dim(
        prenorm_gain, shift_amount, feature_width
    )
    input_row_sums = lax.psum(
        (jnp.sum(scaled_input, axis=1), jnp.sum(scaled_input * centered_input_portion, axis=1)),
        "txt",
    )
    input_gradient = (
        output_gradient
        + (
            scaled_input
            - input_row_sums[0][:, None] / MODEL_WIDTH
            - centered_input_portion * (input_row_sums[1][:, None] / MODEL_WIDTH)
        )
        * input_inverse_deviation
    )
    square_sum = lax.psum(jnp.sum(input_gradient * input_gradient, axis=1), "txt")
    grad_rms = jnp.sqrt(square_sum[:, None] / MODEL_WIDTH + 1e-06)
    return own_rows + step_size[0] * input_gradient / grad_rms


def solution(mesh):
    placed = (
        P("dp", "txt"),
        P(),
        P(),
        P("dp", "txt"),
        P("txt"),
        P("txt", "dp"),
        P(),
        P("txt"),
        P("txt"),
        P("txt", None),
        P("txt", None),
        P("dp"),
        P(),
    )
    return jax.shard_map(
        local, mesh=mesh, in_specs=placed, out_specs=P("dp", "txt"), check_vma=False
    )
```

profile of v0, /device:TPU:0, one launch (start us, length us, event | category | flops | bytes accessed | tf_op | source)
XLA Modules:
  0.0 297.3 jit_solution(12234471146780298693)
XLA Ops:
  8.1 8.9 %all_gather.18 = bf16[256,1024]{1,0:T(8,128)(2,1)S(1)} all-gather(bf16[256,256]{1,0:T(8,128)(2,1)} %param.13), channel_id=1, replica_groups=mesh['dp'=8,'txt'=4] {'txt'}, dimensions={1}, use_global_device_ids=true | all-gather | bytes 655360 | tf_op jit(solution)/shard_map/all_gather | solution.py:26
  17.2 44.1 %all-gather.3.cloned.1.call-done = bf16[1024,1024]{1,0:T(8,128)(2,1)} async-done(((bf16[128,1024]{1,0:T(8,128)(2,1)}), bf16[1024,1024]{1,0:T(8,128)(2,1)}) %all-gather.3.cloned.1.call-update) | async-done | bytes 2097168 | tf_op jit(solution)/shard_map/all_gather | solution.py:33
  61.3 2.4 convolution_add_fusion
  63.7 48.5 %all-gather.5.cloned.1.call-done = bf16[1024,1024]{1,0:T(8,128)(2,1)} async-done(((bf16[1024,128]{1,0:T(8,128)(2,1)}), bf16[1024,1024]{1,0:T(8,128)(2,1)}) %all-gather.5.cloned.1.call-update) | async-done | bytes 2097168 | tf_op jit(solution)/shard_map/all_gather | solution.py:34
  112.3 3.3 %fusion.17 = f32[256,1024]{1,0:T(8,128)} fusion(bf16[1024,1024]{1,0:T(8,128)(2,1)} %all-gather.5.cloned.1.call-done, f32[256,1024]{1,0:T(8,128)S(1)} %convolution_add_fusion), kind=kOutput, calls=%fused_computation.32 | convolution fusion | flops 538443776 | bytes 4194304 | tf_op jit(solution)/shard_map/dot_general | solution.py:38
  115.7 0.9 dynamic_slice.9
  116.6 22.2 %reduce-scatter.5.cloned.1.call-done = f32[256,256]{1,0:T(8,128)} async-done(((f32[256,1024]{1,0:T(8,128)}), f32[256,256]{1,0:T(8,128)}) %reduce-scatter.5.cloned.1.call-update) | async-done | bytes 262160 | tf_op jit(solution)/shard_map/reduce_scatter | solution.py:39
  138.7 1.1 fusion.38
  139.8 5.8 %all-reduce.2 = (f32[256]{0:T(256)S(1)}, f32[256]{0:T(256)S(1)}) all-reduce(f32[256]{0:T(256)S(1)} %get-tuple-element.12, f32[256]{0:T(256)S(1)} %get-tuple-element.11), channel_id=1, replica_groups=mesh['dp'=8,'txt'=4] {'txt'}, use_global_device_ids=true, to_apply=%region_6.0 | all-reduce | flops 512 | bytes 4096 | tf_op jit(solution)/shard_map/psum | solution.py:42
  145.6 1.2 fusion.25
  147.4 1.7 fusion.1
  149.2 21.7 %reduce-scatter.7.cloned.1.call-done = f32[64,768]{1,0:T(8,128)} async-done(((f32[256,768]{1,0:T(8,128)}), f32[64,768]{1,0:T(8,128)}) %reduce-scatter.7.cloned.1.call-update) | async-done | bytes 196624 | tf_op jit(solution)/shard_map/reduce_scatter | solution.py:49
  170.9 1.0 multiply_reduce_fusion.6
  171.9 1.0 fusion.35
  173.0 6.1 %all_gather.21 = bf16[256,768]{1,0:T(8,128)(2,1)S(1)} all-gather(bf16[64,768]{1,0:T(8,128)(2,1)S(1)} %fusion.35), channel_id=1, replica_groups=mesh['dp'=8,'txt'=4] {'txt'}, dimensions={0}, use_global_device_ids=true | all-gather | bytes 491520 | tf_op jit(solution)/shard_map/all_gather | solution.py:52
  179.1 3.5 %fusion.41 = (f32[256]{0:T(256)S(1)}, f32[256,1280]{1,0:T(8,128)}) fusion(bf16[256,768]{1,0:T(8,128)(2,1)S(1)} %all_gather.21, bf16[1280,768]{1,0:T(8,128)(2,1)} %fusion.1), kind=kOutput, calls=%fused_computation.81 | convolution fusion | flops 503971584 | bytes 3671040 | tf_op jit(solution)/shard_map/ie,je->ij/dot_general | solution.py:57
  182.6 6.4 %pmax.7 = f32[256]{0:T(256)S(1)} all-reduce(f32[256]{0:T(256)S(1)} %get-tuple-element.28), channel_id=1, replica_groups=mesh['dp'=8,'txt'=4] {'txt'}, use_global_device_ids=true, to_apply=%region_11.0 | all-reduce | flops 256 | bytes 2048 | tf_op jit(solution)/shard_map/pmax | solution.py:61
  189.0 1.6 fusion.3
  190.7 5.7 %psum.58 = f32[256]{0:T(256)S(1)} all-reduce(f32[256]{0:T(256)S(1)} %fusion.3), channel_id=1, replica_groups=mesh['dp'=8,'txt'=4] {'txt'}, use_global_device_ids=true, to_apply=%region_13.0 | all-reduce | flops 256 | bytes 2048 | tf_op jit(solution)/shard_map/psum | solution.py:63
  196.3 3.2 %fusion.12 = f32[256,768]{1,0:T(8,128)} fusion(bf16[1280,768]{1,0:T(8,128)(2,1)S(1)} %copy-done.2, f32[256,1280]{1,0:T(8,128)} %get-tuple-element.29, s32[256]{0:T(256)S(1)} %broadcast_subtract_fusion, f32[256]{0:T(256)S(1)} %psum.58, f32[256]{0:T(256)S(1)} %pmax.7), kind=kOutput, calls=%fused_computation.27 | convolution fusion | flops 505610240 | bytes 4066304 | tf_op jit(solution)/shard_map/dot_general | solution.py:69
  199.6 23.9 %reduce-scatter.9.cloned.1.call-done = f32[64,768]{1,0:T(8,128)} async-done(((f32[256,768]{1,0:T(8,128)}), f32[64,768]{1,0:T(8,128)}) %reduce-scatter.9.cloned.1.call-update) | async-done | bytes 196624 | tf_op jit(solution)/shard_map/reduce_scatter | solution.py:70
  223.5 1.1 multiply_reduce_fusion.5
  224.6 1.1 divide_convert_fusion
  225.8 6.1 %all_gather.22 = bf16[256,768]{1,0:T(8,128)(2,1)S(1)} all-gather(bf16[64,768]{1,0:T(8,128)(2,1)S(1)} %divide_convert_fusion), channel_id=1, replica_groups=mesh['dp'=8,'txt'=4] {'txt'}, dimensions={0}, use_global_device_ids=true | all-gather | bytes 491520 | tf_op jit(solution)/shard_map/all_gather | solution.py:73
  232.3 6.5 %all-reduce.1 = (f32[256]{0:T(256)S(1)}, f32[256]{0:T(256)S(1)}) all-reduce(f32[256]{0:T(256)S(1)} %get-tuple-element.10, f32[256]{0:T(256)S(1)} %get-tuple-element.9), channel_id=1, replica_groups=mesh['dp'=8,'txt'=4] {'txt'}, use_global_device_ids=true, to_apply=%region_19.0 | all-reduce | flops 512 | bytes 4096 | tf_op jit(solution)/shard_map/psum | solution.py:76
  239.0 6.9 %all_gather.23 = bf16[256,1024]{1,0:T(8,128)(2,1)S(1)} all-gather(bf16[256,256]{1,0:T(8,128)(2,1)S(1)} %get-tuple-element.21), channel_id=1, replica_groups=mesh['dp'=8,'txt'=4] {'txt'}, dimensions={1}, use_global_device_ids=true | all-gather | bytes 655360 | tf_op jit(solution)/shard_map/all_gather | solution.py:80
  245.9 4.7 %fusion.4 = f32[256,1024]{1,0:T(8,128)} fusion(bf16[1024,1024]{1,0:T(8,128)(2,1)} %all-gather.3.cloned.1.call-done, bf16[256,1024]{1,0:T(8,128)(2,1)S(1)} %all_gather.23, bf16[1024,1024]{1,0:T(8,128)(2,1)} %all-gather.5.cloned.1.call-done, f32[256,1024]{1,0:T(8,128)S(1)} %copy-done.9), kind=kOutput, calls=%fused_computation.16 | convolution fusion | flops 1076363264 | bytes 6815744 | tf_op jit(solution)/shard_map/if,df->id/dot_general | solution.py:85
  252.3 23.6 %reduce-scatter.11.cloned.1.call-done = f32[256,256]{1,0:T(8,128)} async-done(((f32[256,1024]{1,0:T(8,128)}), f32[256,256]{1,0:T(8,128)}) %reduce-scatter.11.cloned.1.call-update) | async-done | bytes 262160 | tf_op jit(solution)/shard_map/reduce_scatter | solution.py:86
  275.8 1.1 multiply_reduce_fusion.4
  276.9 5.8 %all-reduce = (f32[256]{0:T(256)S(1)}, f32[256]{0:T(256)S(1)}) all-reduce(f32[256]{0:T(256)S(1)} %get-tuple-element.8, f32[256]{0:T(256)S(1)} %get-tuple-element.7), channel_id=1, replica_groups=mesh['dp'=8,'txt'=4] {'txt'}, use_global_device_ids=true, to_apply=%region_24.0 | all-reduce | flops 512 | bytes 4096 | tf_op jit(solution)/shard_map/psum | solution.py:93
  282.7 1.2 multiply_reduce_fusion
  283.9 5.7 %psum.63 = f32[256]{0:T(256)S(1)} all-reduce(f32[256]{0:T(256)S(1)} %get-tuple-element.19), channel_id=1, replica_groups=mesh['dp'=8,'txt'=4] {'txt'}, use_global_device_ids=true, to_apply=%region_26.0 | all-reduce | flops 256 | bytes 2048 | tf_op jit(solution)/shard_map/psum | solution.py:106
  (48 shorter events, 4.9 us)
Async XLA Ops:
  6.5 139.1 %copy-start = (bf16[256,768]{1,0:T(8,128)(2,1)S(1)}, bf16[256,768]{1,0:T(8,128)(2,1)}, u32[]{:S(2)}) copy-start(bf16[256,768]{1,0:T(8,128)(2,1)} %param.22) | copy-start | bytes 1179652
  6.5 54.8 %all-gather.3.cloned.1.call-start = ((), (), s32[]{:S(2)}) async-start(), calls=%async_computation.4 | async-start | bytes 2359296 | tf_op jit(solution)/shard_map/all_gather | solution.py:33
  7.3 105.0 %all-gather.5.cloned.1.call-start = ((), (), s32[]{:S(2)}) async-start(), calls=%async_computation.5 | async-start | bytes 2359296 | tf_op jit(solution)/shard_map/all_gather | solution.py:34
  8.0 130.7 %reduce-scatter.5.cloned.1.call-start = ((), (), s32[]{:S(2)}) async-start(), calls=%async_computation.6 | async-start | bytes 1310720 | tf_op jit(solution)/shard_map/reduce_scatter | solution.py:39
  63.7 51.9 %copy-start.8 = (f32[256,1024]{1,0:T(8,128)}, f32[256,1024]{1,0:T(8,128)S(1)}, u32[]{:S(2)}) copy-start(f32[256,1024]{1,0:T(8,128)S(1)} %convolution_add_fusion) | copy-start | bytes 3145732
  63.7 75.0 %copy-start.4 = (bf16[256,256]{1,0:T(8,128)(2,1)S(1)}, bf16[256,256]{1,0:T(8,128)(2,1)}, u32[]{:S(2)}) copy-start(bf16[256,256]{1,0:T(8,128)(2,1)} %param.13) | copy-start | bytes 393220
  63.7 81.9 %copy-start.5 = (f32[256]{0:T(256)S(1)}, f32[256]{0:T(256)}, u32[]{:S(2)}) copy-start(f32[256]{0:T(256)} %param.20) | copy-start | bytes 3076
  63.7 81.9 %copy-start.7 = (f32[256]{0:T(256)S(1)}, f32[256]{0:T(256)}, u32[]{:S(2)}) copy-start(f32[256]{0:T(256)} %param.21) | copy-start | bytes 3076
  115.6 31.4 %copy-start.6 = (s32[256]{0:T(256)S(1)}, s32[256]{0:T(256)}, u32[]{:S(2)}) copy-start(s32[256]{0:T(256)} %param.24) | copy-start | bytes 3076
  115.6 31.4 %copy-start.1 = (bf16[1280,768]{1,0:T(8,128)(2,1)S(1)}, bf16[1280,768]{1,0:T(8,128)(2,1)}, u32[]{:S(2)}) copy-start(bf16[1280,768]{1,0:T(8,128)(2,1)} %param.23) | copy-start | bytes 5898244
  115.6 55.3 %reduce-scatter.7.cloned.1.call-start = ((), (), s32[]{:S(2)}) async-start(), calls=%async_computation.7 | async-start | bytes 983040 | tf_op jit(solution)/shard_map/reduce_scatter | solution.py:49
  146.9 76.6 %reduce-scatter.9.cloned.1.call-start = ((), (), s32[]{:S(2)}) async-start(), calls=%async_computation.8 | async-start | bytes 983040 | tf_op jit(solution)/shard_map/reduce_scatter | solution.py:70
  179.1 17.2 %copy-start.2 = (bf16[1280,768]{1,0:T(8,128)(2,1)S(1)}, bf16[1280,768]{1,0:T(8,128)(2,1)}, u32[]{:S(2)}) copy-start(bf16[1280,768]{1,0:T(8,128)(2,1)} %fusion.1) | copy-start | bytes 5898244
  196.3 27.2 %copy-start.3 = (f32[64,768]{1,0:T(8,128)S(1)}, f32[64,768]{1,0:T(8,128)}, u32[]{:S(2)}) copy-start(f32[64,768]{1,0:T(8,128)} %reduce-scatter.7.cloned.1.call-done) | copy-start | bytes 589828
  199.5 76.3 %reduce-scatter.11.cloned.1.call-start = ((), (), s32[]{:S(2)}) async-start(), calls=%async_computation.9 | async-start | bytes 1310720 | tf_op jit(solution)/shard_map/reduce_scatter | solution.py:86
  224.6 21.2 %copy-start.9 = (f32[256,1024]{1,0:T(8,128)S(1)}, f32[256,1024]{1,0:T(8,128)}, u32[]{:S(2)}) copy-start(f32[256,1024]{1,0:T(8,128)} %copy-done.8) | copy-start | bytes 3145732
Sparse Core Ops, SparseCore 0:
  9.5 51.8 all-gather.2
  63.4 48.8 all-gather.4
  115.7 22.9 reduce-scatter.4
  147.0 23.8 reduce-scatter.6
  199.6 23.8 reduce-scatter.8
  250.7 25.0 reduce-scatter.10
where the time goes:
time: 298 us; the launch traced here: 297 us
  waiting for transfers between devices  185 us (62%)
  blocking collectives  63.8 us (21%)
  matrix products  18.7 us (6%)
  between operations  14.3 us (5%)
  other arithmetic  13.1 us (4%)
    all_gather x1, waiting for transfers between devices, local(): w_down = lax.all_gather(down_weight, 'dp', axis=1, tiled=True)  48.5 us
    all_gather x1, waiting for transfers between devices, local(): w_up = lax.all_gather(up_weight, 'dp', axis=0, tiled=True)  44.1 us
    reduce_scatter x1, waiting for transfers between devices, local(): lax.psum_scatter(back_part, 'txt', scatter_dimension=0, tiled=True)  23.9 us
    reduce_scatter x1, waiting for transfers between devices, local(): lax.psum_scatter(normed_part, 'txt', scatter_dimension=1, tiled=True)  23.6 us
    reduce_scatter x1, waiting for transfers between devices, local(): mixed = lax.psum_scatter(mixed_part, 'txt', scatter_dimension=1, tiled=True)  22.2 us
    reduce_scatter x1, waiting for transfers between devices, local(): lax.psum_scatter(emb_part, 'txt', scatter_dimension=0, tiled=True)  21.7 us
    all_gather x1, blocking collectives, local(): gathered = lax.all_gather(resid, 'txt', axis=1, tiled=True)  8.89 us
    all_gather x1, blocking collectives, local(): lax.all_gather(output_gradient.astype(jnp.bfloat16), 'txt', axis=1, tiled...  6.85 us
  transfers between devices with their start and end apart: 6, of which 6 were waited for; matrix products, arithmetic and copies ran while one was open for 2% of the time, Pallas kernels for 0%

commit v1 on v0

v1 whole, which is shorter than its diff:
```python
import functools
import jax
import jax.numpy as jnp
from jax import lax
from jax.experimental import pallas as pl
from jax.experimental.pallas import tpu as pltpu
from jax.sharding import PartitionSpec as P

MESH = pl.DeviceIdType.MESH
F32 = jnp.float32
BF16 = jnp.bfloat16
RESID, PROJ, GAINS, MIXED, UNIT, STATS, BACK, OUTLOW, NORMED, FINAL = range(10)


def nn(a, b):
    return jnp.dot(a, b, preferred_element_type=F32)


def nt_dot(a, b):
    return lax.dot_general(a, b, (((1,), (1,)), ((), ())), preferred_element_type=F32)


def tiles(size, most):
    step = most if size % most == 0 else size
    return size // step, step


def kernel(
    nd, nt,
    resid, pre_gain, pre_bias, up, up_bias, down, down_bias, post_gain, post_bias,
    projection, texts, labels, step_size,
    out,
    rg, xf, normed, wu, wd, wdf, gb_s, gb, gains, pj, tu,
    hidden, dgate, part, ms, mr, us, ug, lg, sg, st_s, st, bpart, bs, br,
    os_, og, ag, ns, nr, ds_, dr,
    send, recv, ring_send, ring_recv,
):
    R, F = resid.shape
    D = nt * F
    Kd, H = up.shape
    E = projection.shape[1]
    T = texts.shape[0]
    r = R // nt
    half = nd // 2
    me = lax.axis_index("txt")
    dpi = lax.axis_index("dp")
    zz = dpi // 2
    xx = dpi % 2
    pos = zz + xx * (nd - 1 - 2 * zz)

    def at_pos(p):
        p = (p + 2 * nd) % nd
        h = p // half
        return 2 * (p + h * (nd - 1 - 2 * p)) + h

    right, left = at_pos(pos + 1), at_pos(pos - 1)

    barrier = pltpu.get_barrier_semaphore()
    for o in range(1, nt):
        pl.semaphore_signal(barrier, inc=1, device_id={"txt": (me + o) % nt}, device_id_type=MESH)
    for nb in (left, right):
        pl.semaphore_signal(barrier, inc=1, device_id={"dp": nb}, device_id_type=MESH)
    pl.semaphore_wait(barrier, nt + 1)

    def tx(which, o, src, dst):
        return pltpu.make_async_remote_copy(
            src_ref=src, dst_ref=dst, send_sem=send.at[which, o - 1], recv_sem=recv.at[which, o - 1],
            device_id={"txt": (me + o) % nt}, device_id_type=MESH)

    def exchange(which, src_of, dst):
        cs = [tx(which, o, src_of((me + o) % nt), dst) for o in range(1, nt)]
        for c in cs:
            c.start()
        return cs

    def finish(cs):
        for c in cs:
            c.wait()

    rows_of = lambda p: pl.ds(pl.multiple_of(p * r, r), r)
    mine = rows_of(me)

    def ring(kind, way, k):
        origin = at_pos(pos - k) if way == 0 else at_pos(pos + k)
        size = Kd if kind == 0 else H
        lo, n = (0, size) if k < half - 1 else ((0, size // 2) if way == 0 else (size // 2, size // 2))
        if kind == 0:
            dst = wu.at[pl.ds(pl.multiple_of(origin * Kd + lo, Kd // 2), n), :]
            src = up.at[pl.ds(lo, n), :] if k == 0 else dst
        else:
            dst = wd.at[origin, pl.ds(lo, n), :]
            src = down.at[pl.ds(lo, n), :] if k == 0 else dst
        return pltpu.make_async_remote_copy(
            src_ref=src, dst_ref=dst, send_sem=ring_send.at[kind, way, k], recv_sem=ring_recv.at[kind, way, k],
            device_id={"dp": right if way == 0 else left}, device_id_type=MESH)

    for kind in range(2):
        for way in range(2):
            ring(kind, way, 0).start()
    c_resid = exchange(RESID, lambda p: resid, rg.at[me])
    gb_s[...] = jnp.zeros_like(gb_s)
    gb_s[0:1, :] = post_gain[...]
    gb_s[1:2, :] = post_bias[...]
    c_gains = exchange(GAINS, lambda p: gb_s, gb.at[me])
    prow = pl.ds(pl.multiple_of(me * F, F), F)
    c_proj = exchange(PROJ, lambda p: projection, pj.at[prow, :])
    rg[me] = resid[...]
    gb[me] = gb_s[...]
    pj[prow, :] = projection[...]
    wu[pl.ds(pl.multiple_of(dpi * Kd, Kd), Kd), :] = up[...]

    def place(s):
        if Kd % 128 == 0:
            wdf[:, pl.ds(pl.multiple_of(s * Kd, Kd), Kd)] = wd[s]

    wd[dpi] = down[...]
    place(dpi)

    tn, tstep = tiles(T, 64)

    @pl.loop(0, tn)
    def _(i):
        sl = pl.ds(pl.multiple_of(i * tstep, tstep), tstep)
        t = texts[sl, :].astype(F32)
        tu[sl, :] = (t / jnp.sqrt(jnp.sum(t * t, axis=1, keepdims=True) + 1e-06)).astype(BF16)

    finish(c_resid)
    for t in range(nt):
        xf[:, t * F:(t + 1) * F] = rg[t].astype(F32)

    def norm_in(x):
        mean = jnp.mean(x, axis=1, keepdims=True)
        var = jnp.mean(x * x, axis=1, keepdims=True) - mean * mean
        rstd = lax.rsqrt(var + 1e-05)
        return (x - mean) * rstd, rstd

    ln, lstep = tiles(R, 64)

    @pl.loop(0, ln)
    def _(i):
        sl = pl.ds(pl.multiple_of(i * lstep, lstep), lstep)
        xhat, _ = norm_in(xf[sl, :])
        normed[sl, :] = (xhat * pre_gain[...] + pre_bias[...]).astype(BF16)

    for k in range(half):
        for kind in range(2):
            if k == half - 1 and kind == 1:
                hn, hstep = tiles(H, 256)

                @pl.loop(0, hn)
                def _(i):
                    sl = pl.ds(pl.multiple_of(i * hstep, hstep), hstep)
                    pre = nn(normed[...], wu[:, sl]) + up_bias[:, sl]
                    sig = jax.nn.sigmoid(1.702 * pre)
                    hidden[:, sl] = (pre * sig).astype(BF16)
                    dgate[:, sl] = sig + 1.702 * pre * sig * (1.0 - sig)

            for way in range(2):
                ring(kind, way, k).wait_recv()
                if k + 1 < half:
                    ring(kind, way, k + 1).start()
            if kind == 1:
                if k < half - 1:
                    place(at_pos(pos - 1 - k))
                    place(at_pos(pos + 1 + k))
                else:
                    place(at_pos(pos + half))
    if Kd % 128 != 0:
        for s in range(nd):
            wdf[:, s * Kd:(s + 1) * Kd] = wd[s]
    for k in range(half):
        for kind in range(2):
            for way in range(2):
                ring(kind, way, k).wait_send()

    dn, dstep = tiles(D, 256)

    @pl.loop(0, dn)
    def _(i):
        sl = pl.ds(pl.multiple_of(i * dstep, dstep), dstep)
        v = nn(hidden[...], wdf[:, sl])
        part[:, sl] = v
        ms[:, sl] = v.astype(BF16)

    c_mixed = exchange(MIXED, lambda p: ms.at[rows_of(p), :], mr.at[me])
    finish(c_gains)
    for t in range(nt):
        gains[:, t * F:(t + 1) * F] = gb[t]
    x_own = xf[mine, :]
    xhat_own, rstd_in = norm_in(x_own)
    block = x_own + down_bias[...] + part[mine, :]
    finish(c_mixed)
    for o in range(1, nt):
        block = block + mr[(me + o) % nt].astype(F32)
    yhat, rstd_out = norm_in(block)
    post_normed = (yhat * gains[0:1, :] + gains[1:2, :]).astype(BF16)
    finish(c_proj)
    emb = nn(post_normed, pj[...])
    emb_norm = jnp.sqrt(jnp.sum(emb * emb, axis=1, keepdims=True) + 1e-06)
    unit = emb / emb_norm
    us[...] = unit.astype(BF16)
    c_unit = exchange(UNIT, lambda p: us, ug.at[mine, :])
    ug[mine, :] = us[...]
    finish(c_unit)

    kn, kstep = tiles(T, 256)

    def logit_tile(i, m):
        sl = pl.ds(pl.multiple_of(i * kstep, kstep), kstep)
        l = 100.0 * nt_dot(ug[...], tu[sl, :])
        lg[:, sl] = l
        return jnp.maximum(m, jnp.max(l, axis=1, keepdims=True))

    top = lax.fori_loop(0, kn, logit_tile, jnp.full((R, 1), -jnp.inf, F32))

    def exp_tile(i, s):
        sl = pl.ds(pl.multiple_of(i * kstep, kstep), kstep)
        e = jnp.exp(lg[:, sl] - top)
        lg[:, sl] = e
        return s + jnp.sum(e, axis=1, keepdims=True)

    total = lax.fori_loop(0, kn, exp_tile, jnp.zeros((R, 1), F32))
    lane = lax.broadcasted_iota(jnp.int32, (R, 128), 1)
    packed = jnp.where(lane == 0, top, total)
    st_s[...] = packed.T[0:8, :]
    c_stats = exchange(STATS, lambda p: st_s, st.at[me])
    st[me] = st_s[...]
    finish(c_stats)
    allm = st[0, 0:1, :]
    for t in range(1, nt):
        allm = jnp.maximum(allm, st[t, 0:1, :])
    alls = jnp.zeros_like(allm)
    for t in range(nt):
        alls = alls + st[t, 1:2, :] * jnp.exp(st[t, 0:1, :] - allm)
    row = lax.broadcasted_iota(jnp.int32, (128, R), 0)
    back_t = jnp.where(row == 0, allm, alls).T
    factor = jnp.exp(top - back_t[:, 0:1]) / back_t[:, 1:2]
    local_label = labels[...] - me * T

    @pl.loop(0, kn)
    def _(i):
        sl = pl.ds(pl.multiple_of(i * kstep, kstep), kstep)
        prob = lg[:, sl] * factor
        cols = lax.broadcasted_iota(jnp.int32, (R, kstep), 1) + i * kstep
        target = (cols == local_label).astype(F32)
        sg[:, sl] = (100.0 * (prob - target)).astype(BF16)

    en, estep = tiles(E, 256)

    @pl.loop(0, en)
    def _(i):
        sl = pl.ds(pl.multiple_of(i * estep, estep), estep)
        v = nn(sg[...], tu[:, sl])
        bpart[:, sl] = v
        bs[:, sl] = v.astype(BF16)

    c_back = exchange(BACK, lambda p: bs.at[rows_of(p), :], br.at[me])
    ugrad = bpart[mine, :]
    finish(c_back)
    for o in range(1, nt):
        ugrad = ugrad + br[(me + o) % nt].astype(F32)
    along = jnp.sum(unit * ugrad, axis=1, keepdims=True)
    emb_grad = ((ugrad - unit * along) / emb_norm).astype(BF16)

    def norm_back(scaled, hat, rstd):
        first = jnp.mean(scaled, axis=1, keepdims=True)
        second = jnp.mean(scaled * hat, axis=1, keepdims=True)
        return (scaled - first - hat * second) * rstd

    out_grad = norm_back(nt_dot(emb_grad, pj[...]) * gains[0:1, :], yhat, rstd_out)
    os_[...] = out_grad.astype(BF16)
    c_out = exchange(OUTLOW, lambda p: os_, og.at[mine, :])
    og[mine, :] = os_[...]
    finish(c_out)
    hn, hstep = tiles(H, 256)

    @pl.loop(0, hn)
    def _(i):
        sl = pl.ds(pl.multiple_of(i * hstep, hstep), hstep)
        ag[:, sl] = (nt_dot(og[...], wdf[sl, :]) * dgate[:, sl]).astype(BF16)

    @pl.loop(0, dn)
    def _(i):
        sl = pl.ds(pl.multiple_of(i * dstep, dstep), dstep)
        v = nt_dot(ag[...], wu[sl, :])
        part[:, sl] = v
        ns[:, sl] = v.astype(BF16)

    c_norm = exchange(NORMED, lambda p: ns.at[rows_of(p), :], nr.at[me])
    ngrad = part[mine, :]
    finish(c_norm)
    for o in range(1, nt):
        ngrad = ngrad + nr[(me + o) % nt].astype(F32)
    in_grad = out_grad + norm_back(ngrad * pre_gain[...], xhat_own, rstd_in)
    rms = jnp.sqrt(jnp.mean(in_grad * in_grad, axis=1, keepdims=True) + 1e-06)
    delta = step_size[0] * in_grad / rms
    for t in range(nt):
        ds_[t] = delta[:, t * F:(t + 1) * F]
    c_fin = exchange(FINAL, lambda p: ds_.at[p], dr.at[mine, :])
    dr[mine, :] = ds_[me]
    finish(c_fin)
    out[...] = resid[...].astype(F32) + dr[...]


def solution(mesh):
    nd, nt = mesh.shape["dp"], mesh.shape["txt"]
    placed = (
        P("dp", "txt"),
        P(),
        P(),
        P("dp", "txt"),
        P("txt"),
        P("txt", "dp"),
        P(),
        P("txt"),
        P("txt"),
        P("txt", None),
        P("txt", None),
        P("dp"),
        P(),
    )

    def local(resid, pre_gain, pre_bias, up, up_bias, down, down_bias, post_gain, post_bias,
              projection, texts, labels, step_size):
        R, F = resid.shape
        D = nt * F
        Kd, H = up.shape
        E = projection.shape[1]
        T = texts.shape[0]
        r = R // nt
        V = pltpu.VMEM
        scratch = [
            V((nt, R, F), BF16),
            V((R, D), F32),
            V((R, D), BF16),
            V((D, H), BF16),
            V((nd, H, Kd), BF16),
            V((H, D), BF16),
            V((8, F), F32),
            V((nt, 8, F), F32),
            V((8, D), F32),
            V((D, E), BF16),
            V((T, E), BF16),
            V((R, H), BF16),
            V((R, H), F32),
            V((R, D), F32),
            V((R, D), BF16),
            V((nt, r, D), BF16),
            V((r, E), BF16),
            V((R, E), BF16),
            V((R, T), F32),
            V((R, T), BF16),
            V((8, R), F32),
            V((nt, 8, R), F32),
            V((R, E), F32),
            V((R, E), BF16),
            V((nt, r, E), BF16),
            V((r, D), BF16),
            V((R, D), BF16),
            V((R, H), BF16),
            V((R, D), BF16),
            V((nt, r, D), BF16),
            V((nt, r, F), F32),
            V((R, F), F32),
            pltpu.SemaphoreType.DMA((10, nt - 1)),
            pltpu.SemaphoreType.DMA((10, nt - 1)),
            pltpu.SemaphoreType.DMA((2, 2, nd // 2)),
            pltpu.SemaphoreType.DMA((2, 2, nd // 2)),
        ]
        vm = pl.BlockSpec(memory_space=pltpu.VMEM)
        line = lambda v: v.reshape(1, -1)
        return pl.pallas_call(
            functools.partial(kernel, nd, nt),
            out_shape=jax.ShapeDtypeStruct((R, F), F32),
            in_specs=[vm] * 12 + [pl.BlockSpec(memory_space=pltpu.SMEM)],
            out_specs=vm,
            scratch_shapes=scratch,
            compiler_params=pltpu.CompilerParams(
                collective_id=0, has_side_effects=True, vmem_limit_bytes=60 * 1024 * 1024),
        )(resid, line(pre_gain), line(pre_bias), up, line(up_bias), down, line(down_bias),
          line(post_gain), line(post_bias), projection, texts, labels.reshape(-1, 1), step_size)

    return jax.shard_map(local, mesh=mesh, in_specs=placed, out_specs=P("dp", "txt"), check_vma=False)
```

time: 298 us -> 98.6 us (0.33)
  waiting for transfers between devices: 185 us -> 0 us
  Pallas kernels: 0 us -> 94.5 us
  blocking collectives: 63.8 us -> 0 us
  matrix products: 18.7 us -> 0 us
  between operations: 14.3 us -> 0.66 us
  other arithmetic: 13.1 us -> 0 us
    pallas_call x0 -> x1, Pallas kernels: none -> 94.5 us  [local(): pl.pallas_call(functools.partial(kernel, nd, nt), out_shape=jax.ShapeDtyp...]
    all_gather x2 -> x0, waiting for transfers between devices: 92.6 us -> none  [the longest x1 48.5 us: local(): w_down = lax.all_gather(down_weight, 'dp', axis=1, tiled=True)]
    reduce_scatter x4 -> x0, waiting for transfers between devices: 91.4 us -> none  [the longest x1 23.9 us: local(): lax.psum_scatter(back_part, 'txt', scatter_dimension=0, tiled=True)]
    psum x5 -> x0, blocking collectives: 29.3 us -> none  [the longest x1 6.45 us: local(): lax.psum((jnp.sum(scaled, axis=1), jnp.sum(scaled * yhat, axis=1)), 'txt')]
    all_gather x4 -> x0, blocking collectives: 28 us -> none  [the longest x1 8.89 us: local(): gathered = lax.all_gather(resid, 'txt', axis=1, tiled=True)]
    dot_general x7 -> x0, matrix products: 18.7 us -> none  [the longest x1 4.72 us: local(): jnp.einsum('if,df->id', act_grad, w_up, preferred_element_type=jnp.float32)]
    reduce_sum x8 -> x0, other arithmetic: 7.89 us -> none  [the longest x1 1.64 us: local(): row_total = lax.psum(jnp.sum(exponent, axis=1), 'txt')]
    pmax x1 -> x0, blocking collectives: 6.42 us -> none  [local(): row_top = lax.pmax(local_top, 'txt')]
  transfers between devices with their start and end apart: 6 -> 0, of which waited for: 6 -> 0; matrix products, arithmetic and copies ran while one was open for 2% -> 0% of each run, Pallas kernels for 0% -> 0%
where the time goes in v1:
time: 98.6 us; the launch traced here: 98.3 us
  Pallas kernels  94.5 us (96%)
  local copies, waits for them, and re-layouts  3.14 us (3%)
    pallas_call x1, Pallas kernels, local(): pl.pallas_call(functools.partial(kernel, nd, nt), out_shape=jax.ShapeDtyp...  94.5 us

profile of v1, /device:TPU:0, one launch (start us, length us, event | category | flops | bytes accessed | tf_op | source)
XLA Modules:
  0.0 98.3 jit_solution(6166661141826049938)
XLA Ops:
  0.7 1.5 %copy.14.labels = s32[256,1]{1,0:T(8,128)} copy(s32[256,1]{0,1:T(1,128)} %bitcast.13) | data formatting | bytes 2048 | tf_op jit(solution)/shard_map/reshape | solution.py:381
  2.1 94.5 %shard_map.127 = f32[256,256]{1,0:T(8,128)} custom-call(bf16[256,256]{1,0:T(8,128)(2,1)} %resid.1, f32[1,1024]{1,0:T(1,128)} %bitcast.7, f32[1,1024]{1,0:T(1,128)} %bitcast.8, bf16[128,1024]{1,0:T(8,128)(2,1)} %up.1, f32[1,1024]{1,0:T(1,128)} %bitcast.9, bf16[1024,128]{1,0:T(8,128)(2,1)} %down.1, f32[1,1024]{1,0:T(1,128)} %bitcast.10, f32[1,256]{1,0:T(1,128)} %bitcast.11, ...), custom_call_target="tpu_custom_call" | custom-call | tf_op jit(solution)/shard_map/pallas_call | solution.py:372
  96.7 1.7 %copy.17 = f32[256,256]{1,0:T(8,128)} copy(f32[256,256]{1,0:T(8,128)} %shard_map.127) | data formatting | bytes 524288

commit v2 on v1

v2 whole, which is shorter than its diff:
```python
import functools
import jax
import jax.numpy as jnp
from jax import lax
from jax.experimental import pallas as pl
from jax.experimental.pallas import tpu as pltpu
from jax.sharding import PartitionSpec as P

MESH = pl.DeviceIdType.MESH
F32 = jnp.float32
BF16 = jnp.bfloat16
RESID, PROJ, GAINS, MIXED, UNIT, STATS, BACK, OUTLOW, NORMED, FINAL = range(10)


def nn(a, b):
    return jnp.dot(a, b, preferred_element_type=F32)


def nt_dot(a, b):
    return lax.dot_general(a, b, (((1,), (1,)), ((), ())), preferred_element_type=F32)


def tiles(size, most):
    step = most if size % most == 0 else size
    return size // step, step


def halves(r):
    return 2 if r % 32 == 0 else 1


def kernel(
    nd, nt,
    resid, pre_gain, pre_bias, up, up_bias, down, down_bias, post_gain, post_bias,
    projection, texts, labels, step_size,
    out,
    rg, xf, normed, wu, wd, wdf, gb_s, gb, gains, pj, tu,
    hidden, dgate, part, ms, mr, us, ug, lg, sg, st_s, st, bpart, bs, br,
    os_, og, ag, ns, nr, ds_, dr,
    lab, traw, text_sem, send, recv, ring_send, ring_recv,
):
    R, F = resid.shape
    D = nt * F
    Kd, H = up.shape
    E = projection.shape[1]
    T = texts.shape[0]
    r = R // nt
    NH = halves(r)
    rh, Rh = r // NH, R // NH
    half = nd // 2
    me = lax.axis_index("txt")
    dpi = lax.axis_index("dp")
    zz = dpi // 2
    xx = dpi % 2
    pos = zz + xx * (nd - 1 - 2 * zz)

    def at_pos(p):
        p = (p + 2 * nd) % nd
        h = p // half
        return 2 * (p + h * (nd - 1 - 2 * p)) + h

    right, left = at_pos(pos + 1), at_pos(pos - 1)

    text_copy = pltpu.make_async_copy(texts, traw, text_sem)
    text_copy.start()
    barrier = pltpu.get_barrier_semaphore()
    for o in range(1, nt):
        pl.semaphore_signal(barrier, inc=1, device_id={"txt": (me + o) % nt}, device_id_type=MESH)
    for nb in (left, right):
        pl.semaphore_signal(barrier, inc=1, device_id={"dp": nb}, device_id_type=MESH)
    pl.semaphore_wait(barrier, nt + 1)

    def tx(which, h, o, src, dst):
        return pltpu.make_async_remote_copy(
            src_ref=src, dst_ref=dst, send_sem=send.at[h, which, o - 1], recv_sem=recv.at[h, which, o - 1],
            device_id={"txt": (me + o) % nt}, device_id_type=MESH)

    def exchange(which, src_of, dst, h=0):
        cs = [tx(which, h, o, src_of((me + o) % nt), dst) for o in range(1, nt)]
        for c in cs:
            c.start()
        return cs

    def finish(cs):
        for c in cs:
            c.wait()

    in_half = lambda p: pl.ds(pl.multiple_of(p * rh, rh), rh)
    rows_of = lambda h, p: pl.ds(pl.multiple_of(h * Rh + p * rh, rh), rh)
    whole_half = lambda h: pl.ds(h * Rh, Rh)

    def ring(kind, way, k):
        origin = at_pos(pos - k) if way == 0 else at_pos(pos + k)
        size = Kd if kind == 0 else H
        lo, n = (0, size) if k < half - 1 else ((0, size // 2) if way == 0 else (size // 2, size // 2))
        if kind == 0:
            dst = wu.at[pl.ds(pl.multiple_of(origin * Kd + lo, Kd // 2), n), :]
            src = up.at[pl.ds(lo, n), :] if k == 0 else dst
        else:
            dst = wd.at[origin, pl.ds(lo, n), :]
            src = down.at[pl.ds(lo, n), :] if k == 0 else dst
        return pltpu.make_async_remote_copy(
            src_ref=src, dst_ref=dst, send_sem=ring_send.at[kind, way, k], recv_sem=ring_recv.at[kind, way, k],
            device_id={"dp": right if way == 0 else left}, device_id_type=MESH)

    for kind in range(2):
        for way in range(2):
            ring(kind, way, 0).start()
    c_resid = exchange(RESID, lambda p: resid, rg.at[me])
    gb_s[...] = jnp.zeros_like(gb_s)
    gb_s[0:1, :] = post_gain[...]
    gb_s[1:2, :] = post_bias[...]
    c_gains = exchange(GAINS, lambda p: gb_s, gb.at[me])
    prow = pl.ds(pl.multiple_of(me * F, F), F)
    c_proj = exchange(PROJ, lambda p: projection, pj.at[prow, :])
    rg[me] = resid[...]
    gb[me] = gb_s[...]
    pj[prow, :] = projection[...]
    wu[pl.ds(pl.multiple_of(dpi * Kd, Kd), Kd), :] = up[...]

    def place(s):
        if Kd % 128 == 0:
            wdf[:, pl.ds(pl.multiple_of(s * Kd, Kd), Kd)] = wd[s]

    wd[dpi] = down[...]
    place(dpi)

    lab_t = jnp.broadcast_to(labels[...].astype(F32), (128, R)).T
    for h in range(NH):
        for p in range(nt):
            q, n = h * Rh + p * rh, p * r + h * rh
            lab[q:q + rh, :] = lab_t[n:n + rh, :]

    text_copy.wait()
    tn, tstep = tiles(T, 64)

    @pl.loop(0, tn)
    def _(i):
        sl = pl.ds(pl.multiple_of(i * tstep, tstep), tstep)
        t = traw[sl, :].astype(F32)
        tu[sl, :] = (t / jnp.sqrt(jnp.sum(t * t, axis=1, keepdims=True) + 1e-06)).astype(BF16)

    finish(c_resid)
    for t in range(nt):
        for h in range(NH):
            for p in range(nt):
                q, n = h * Rh + p * rh, p * r + h * rh
                xf[q:q + rh, t * F:(t + 1) * F] = rg[t, n:n + rh, :].astype(F32)

    def norm_in(x):
        mean = jnp.mean(x, axis=1, keepdims=True)
        var = jnp.mean(x * x, axis=1, keepdims=True) - mean * mean
        rstd = lax.rsqrt(var + 1e-05)
        return (x - mean) * rstd, rstd

    ln, lstep = tiles(R, 64)

    @pl.loop(0, ln)
    def _(i):
        sl = pl.ds(pl.multiple_of(i * lstep, lstep), lstep)
        xhat, _ = norm_in(xf[sl, :])
        normed[sl, :] = (xhat * pre_gain[...] + pre_bias[...]).astype(BF16)

    for k in range(half):
        for kind in range(2):
            if k == half - 1 and kind == 1:
                hn, hstep = tiles(H, 256)

                @pl.loop(0, hn)
                def _(i):
                    sl = pl.ds(pl.multiple_of(i * hstep, hstep), hstep)
                    pre = nn(normed[...], wu[:, sl]) + up_bias[:, sl]
                    sig = jax.nn.sigmoid(1.702 * pre)
                    hidden[:, sl] = (pre * sig).astype(BF16)
                    dgate[:, sl] = sig + 1.702 * pre * sig * (1.0 - sig)

            for way in range(2):
                ring(kind, way, k).wait_recv()
                if k + 1 < half:
                    ring(kind, way, k + 1).start()
            if kind == 1:
                if k < half - 1:
                    place(at_pos(pos - 1 - k))
                    place(at_pos(pos + 1 + k))
                else:
                    place(at_pos(pos + half))
    if Kd % 128 != 0:
        for s in range(nd):
            wdf[:, s * Kd:(s + 1) * Kd] = wd[s]
    for k in range(half):
        for kind in range(2):
            for way in range(2):
                ring(kind, way, k).wait_send()

    dn, dstep = tiles(D, 256)
    hn, hstep = tiles(H, 256)
    kn, kstep = tiles(T, 256)
    en, estep = tiles(E, 256)
    both = range(NH)
    c_mixed, c_unit, c_stats, c_back, c_out, c_norm, c_fin = ([None] * NH for _ in range(7))
    xhat_own, rstd_in, yhat, rstd_out, unit, emb_norm, out_grad, tops = ([None] * NH for _ in range(8))

    def norm_back(scaled, hat, rstd):
        first = jnp.mean(scaled, axis=1, keepdims=True)
        second = jnp.mean(scaled * hat, axis=1, keepdims=True)
        return (scaled - first - hat * second) * rstd

    for h in both:
        hs = whole_half(h)

        @pl.loop(0, dn)
        def _(i):
            sl = pl.ds(pl.multiple_of(i * dstep, dstep), dstep)
            v = nn(hidden[hs, :], wdf[:, sl])
            part[hs, sl] = v
            ms[hs, sl] = v.astype(BF16)

        c_mixed[h] = exchange(MIXED, lambda p: ms.at[rows_of(h, p), :], mr.at[h, me], h)

    finish(c_gains)
    for t in range(nt):
        gains[:, t * F:(t + 1) * F] = gb[t]

    for h in both:
        own = rows_of(h, me)
        x_own = xf[own, :]
        xhat_own[h], rstd_in[h] = norm_in(x_own)
        block = x_own + down_bias[...] + part[own, :]
        finish(c_mixed[h])
        for o in range(1, nt):
            block = block + mr[h, (me + o) % nt].astype(F32)
        yhat[h], rstd_out[h] = norm_in(block)
        post_normed = (yhat[h] * gains[0:1, :] + gains[1:2, :]).astype(BF16)
        if h == 0:
            finish(c_proj)
        emb = nn(post_normed, pj[...])
        emb_norm[h] = jnp.sqrt(jnp.sum(emb * emb, axis=1, keepdims=True) + 1e-06)
        unit[h] = emb / emb_norm[h]
        us[h] = unit[h].astype(BF16)
        c_unit[h] = exchange(UNIT, lambda p: us.at[h], ug.at[own, :], h)
        ug[own, :] = us[h]

    for h in both:
        hs = whole_half(h)
        finish(c_unit[h])

        def logit_tile(i, m):
            sl = pl.ds(pl.multiple_of(i * kstep, kstep), kstep)
            l = 100.0 * nt_dot(ug[hs, :], tu[sl, :])
            lg[hs, sl] = l
            return jnp.maximum(m, jnp.max(l, axis=1, keepdims=True))

        top = lax.fori_loop(0, kn, logit_tile, jnp.full((Rh, 1), -jnp.inf, F32))

        def exp_tile(i, s):
            sl = pl.ds(pl.multiple_of(i * kstep, kstep), kstep)
            e = jnp.exp(lg[hs, sl] - top)
            lg[hs, sl] = e
            return s + jnp.sum(e, axis=1, keepdims=True)

        total = lax.fori_loop(0, kn, exp_tile, jnp.zeros((Rh, 1), F32))
        tops[h] = top
        lane = lax.broadcasted_iota(jnp.int32, (Rh, 128), 1)
        st_s[h] = jnp.where(lane == 0, top, total).T[0:8, :]
        c_stats[h] = exchange(STATS, lambda p: st_s.at[h], st.at[h, me], h)
        st[h, me] = st_s[h]

    for h in both:
        hs = whole_half(h)
        local_label = lab[hs, 0:1] - (me * T).astype(F32)
        finish(c_stats[h])
        allm = st[h, 0, 0:1, :]
        for t in range(1, nt):
            allm = jnp.maximum(allm, st[h, t, 0:1, :])
        alls = jnp.zeros_like(allm)
        for t in range(nt):
            alls = alls + st[h, t, 1:2, :] * jnp.exp(st[h, t, 0:1, :] - allm)
        row = lax.broadcasted_iota(jnp.int32, (128, Rh), 0)
        back_t = jnp.where(row == 0, allm, alls).T
        factor = jnp.exp(tops[h] - back_t[:, 0:1]) / back_t[:, 1:2]

        @pl.loop(0, kn)
        def _(i):
            sl = pl.ds(pl.multiple_of(i * kstep, kstep), kstep)
            prob = lg[hs, sl] * factor
            cols = (lax.broadcasted_iota(jnp.int32, (Rh, kstep), 1) + i * kstep).astype(F32)
            target = (cols == local_label).astype(F32)
            sg[hs, sl] = (100.0 * (prob - target)).astype(BF16)

        @pl.loop(0, en)
        def _(i):
            sl = pl.ds(pl.multiple_of(i * estep, estep), estep)
            v = nn(sg[hs, :], tu[:, sl])
            bpart[hs, sl] = v
            bs[hs, sl] = v.astype(BF16)

        c_back[h] = exchange(BACK, lambda p: bs.at[rows_of(h, p), :], br.at[h, me], h)

    for h in both:
        own = rows_of(h, me)
        ugrad = bpart[own, :]
        finish(c_back[h])
        for o in range(1, nt):
            ugrad = ugrad + br[h, (me + o) % nt].astype(F32)
        along = jnp.sum(unit[h] * ugrad, axis=1, keepdims=True)
        emb_grad = ((ugrad - unit[h] * along) / emb_norm[h]).astype(BF16)
        out_grad[h] = norm_back(nt_dot(emb_grad, pj[...]) * gains[0:1, :], yhat[h], rstd_out[h])
        os_[h] = out_grad[h].astype(BF16)
        c_out[h] = exchange(OUTLOW, lambda p: os_.at[h], og.at[own, :], h)
        og[own, :] = os_[h]

    for h in both:
        hs = whole_half(h)
        finish(c_out[h])

        @pl.loop(0, hn)
        def _(i):
            sl = pl.ds(pl.multiple_of(i * hstep, hstep), hstep)
            ag[hs, sl] = (nt_dot(og[hs, :], wdf[sl, :]) * dgate[hs, sl]).astype(BF16)

        @pl.loop(0, dn)
        def _(i):
            sl = pl.ds(pl.multiple_of(i * dstep, dstep), dstep)
            v = nt_dot(ag[hs, :], wu[sl, :])
            part[hs, sl] = v
            ns[hs, sl] = v.astype(BF16)

        c_norm[h] = exchange(NORMED, lambda p: ns.at[rows_of(h, p), :], nr.at[h, me], h)

    for h in both:
        ngrad = part[rows_of(h, me), :]
        finish(c_norm[h])
        for o in range(1, nt):
            ngrad = ngrad + nr[h, (me + o) % nt].astype(F32)
        in_grad = out_grad[h] + norm_back(ngrad * pre_gain[...], xhat_own[h], rstd_in[h])
        rms = jnp.sqrt(jnp.mean(in_grad * in_grad, axis=1, keepdims=True) + 1e-06)
        delta = step_size[0] * in_grad / rms
        for t in range(nt):
            ds_[h, t] = delta[:, t * F:(t + 1) * F]
        land = pl.ds(pl.multiple_of(me * r + h * rh, rh), rh)
        c_fin[h] = exchange(FINAL, lambda p: ds_.at[h, p], dr.at[land, :], h)
        dr[land, :] = ds_[h, me]
    for h in both:
        finish(c_fin[h])
    out[...] = resid[...].astype(F32) + dr[...]


def solution(mesh):
    nd, nt = mesh.shape["dp"], mesh.shape["txt"]
    placed = (
        P("dp", "txt"),
        P(),
        P(),
        P("dp", "txt"),
        P("txt"),
        P("txt", "dp"),
        P(),
        P("txt"),
        P("txt"),
        P("txt", None),
        P("txt", None),
        P("dp"),
        P(),
    )

    def local(resid, pre_gain, pre_bias, up, up_bias, down, down_bias, post_gain, post_bias,
              projection, texts, labels, step_size):
        R, F = resid.shape
        D = nt * F
        Kd, H = up.shape
        E = projection.shape[1]
        T = texts.shape[0]
        r = R // nt
        NH = halves(r)
        rh, Rh = r // NH, R // NH
        V = pltpu.VMEM
        scratch = [
            V((nt, R, F), BF16),
            V((R, D), F32),
            V((R, D), BF16),
            V((D, H), BF16),
            V((nd, H, Kd), BF16),
            V((H, D), BF16),
            V((8, F), F32),
            V((nt, 8, F), F32),
            V((8, D), F32),
            V((D, E), BF16),
            V((T, E), BF16),
            V((R, H), BF16),
            V((R, H), F32),
            V((R, D), F32),
            V((R, D), BF16),
            V((NH, nt, rh, D), BF16),
            V((NH, rh, E), BF16),
            V((R, E), BF16),
            V((R, T), F32),
            V((R, T), BF16),
            V((NH, 8, Rh), F32),
            V((NH, nt, 8, Rh), F32),
            V((R, E), F32),
            V((R, E), BF16),
            V((NH, nt, rh, E), BF16),
            V((NH, rh, D), BF16),
            V((R, D), BF16),
            V((R, H), BF16),
            V((R, D), BF16),
            V((NH, nt, rh, D), BF16),
            V((NH, nt, rh, F), F32),
            V((R, F), F32),
            V((R, 128), F32),
            V((T, E), BF16),
            pltpu.SemaphoreType.DMA,
            pltpu.SemaphoreType.DMA((NH, 10, nt - 1)),
            pltpu.SemaphoreType.DMA((NH, 10, nt - 1)),
            pltpu.SemaphoreType.DMA((2, 2, nd // 2)),
            pltpu.SemaphoreType.DMA((2, 2, nd // 2)),
        ]
        vm = pl.BlockSpec(memory_space=pltpu.VMEM)
        line = lambda v: v.reshape(1, -1)
        return pl.pallas_call(
            functools.partial(kernel, nd, nt),
            out_shape=jax.ShapeDtypeStruct((R, F), F32),
            in_specs=[vm] * 10 + [pl.BlockSpec(memory_space=pl.ANY), vm] + [pl.BlockSpec(memory_space=pltpu.SMEM)],
            out_specs=vm,
            scratch_shapes=scratch,
            compiler_params=pltpu.CompilerParams(
                collective_id=0, has_side_effects=True, vmem_limit_bytes=60 * 1024 * 1024),
        )(resid, line(pre_gain), line(pre_bias), up, line(up_bias), down, line(down_bias),
          line(post_gain), line(post_bias), projection, texts, line(labels), step_size)

    return jax.shard_map(local, mesh=mesh, in_specs=placed, out_specs=P("dp", "txt"), check_vma=False)
```

time: 98.6 us -> 89.2 us (0.905)
  Pallas kernels: 94.5 us -> 86.7 us
  local copies, waits for them, and re-layouts: 3.14 us -> 1.67 us
    pallas_call x1, Pallas kernels: 94.5 us -> 86.7 us  [local(): pl.pallas_call(functools.partial(kernel, nd, nt), out_shape=jax.ShapeDtyp...]
    reshape x1 -> x0, local copies, waits for them, and re-layouts: 1.47 us -> none  [local(): labels.reshape(-1, 1)]
where the time goes in v2:
time: 89.2 us; the launch traced here: 89 us
  Pallas kernels  86.7 us (97%)
  local copies, waits for them, and re-layouts  1.67 us (2%)
    pallas_call x1, Pallas kernels, local(): pl.pallas_call(functools.partial(kernel, nd, nt), out_shape=jax.ShapeDtyp...  86.7 us

profile of v2, /device:TPU:0, one launch (start us, length us, event | category | flops | bytes accessed | tf_op | source)
XLA Modules:
  0.0 89.0 jit_solution(16720134692626053288)
XLA Ops:
  0.7 86.7 %shard_map.127 = f32[256,256]{1,0:T(8,128)} custom-call(bf16[256,256]{1,0:T(8,128)(2,1)} %resid.1, f32[1,1024]{1,0:T(1,128)} %bitcast.7, f32[1,1024]{1,0:T(1,128)} %bitcast.8, bf16[128,1024]{1,0:T(8,128)(2,1)} %up.1, f32[1,1024]{1,0:T(1,128)} %bitcast.9, bf16[1024,128]{1,0:T(8,128)(2,1)} %down.1, f32[1,1024]{1,0:T(1,128)} %bitcast.10, f32[1,256]{1,0:T(1,128)} %bitcast.11, ...), custom_call_target="tpu_custom_call" | custom-call | tf_op jit(solution)/shard_map/pallas_call | solution.py:420
  87.3 1.7 %copy.16 = f32[256,256]{1,0:T(8,128)} copy(f32[256,256]{1,0:T(8,128)} %shard_map.127) | data formatting | bytes 524288

commit v3 on v2

--- a/solution.py
+++ b/solution.py
@@ -166,7 +166,7 @@
             if k == half - 1 and kind == 1:
                 hn, hstep = tiles(H, 256)
 
-                @pl.loop(0, hn)
+                @pl.loop(0, hn, unroll=True)
                 def _(i):
                     sl = pl.ds(pl.multiple_of(i * hstep, hstep), hstep)
                     pre = nn(normed[...], wu[:, sl]) + up_bias[:, sl]
@@ -208,7 +208,7 @@
     for h in both:
         hs = whole_half(h)
 
-        @pl.loop(0, dn)
+        @pl.loop(0, dn, unroll=True)
         def _(i):
             sl = pl.ds(pl.multiple_of(i * dstep, dstep), dstep)
             v = nn(hidden[hs, :], wdf[:, sl])
@@ -250,7 +250,7 @@
             lg[hs, sl] = l
             return jnp.maximum(m, jnp.max(l, axis=1, keepdims=True))
 
-        top = lax.fori_loop(0, kn, logit_tile, jnp.full((Rh, 1), -jnp.inf, F32))
+        top = lax.fori_loop(0, kn, logit_tile, jnp.full((Rh, 1), -jnp.inf, F32), unroll=True)
 
         def exp_tile(i, s):
             sl = pl.ds(pl.multiple_of(i * kstep, kstep), kstep)
@@ -258,7 +258,7 @@
             lg[hs, sl] = e
             return s + jnp.sum(e, axis=1, keepdims=True)
 
-        total = lax.fori_loop(0, kn, exp_tile, jnp.zeros((Rh, 1), F32))
+        total = lax.fori_loop(0, kn, exp_tile, jnp.zeros((Rh, 1), F32), unroll=True)
         tops[h] = top
         lane = lax.broadcasted_iota(jnp.int32, (Rh, 128), 1)
         st_s[h] = jnp.where(lane == 0, top, total).T[0:8, :]
@@ -279,7 +279,7 @@
         back_t = jnp.where(row == 0, allm, alls).T
         factor = jnp.exp(tops[h] - back_t[:, 0:1]) / back_t[:, 1:2]
 
-        @pl.loop(0, kn)
+        @pl.loop(0, kn, unroll=True)
         def _(i):
             sl = pl.ds(pl.multiple_of(i * kstep, kstep), kstep)
             prob = lg[hs, sl] * factor
@@ -287,7 +287,7 @@
             target = (cols == local_label).astype(F32)
             sg[hs, sl] = (100.0 * (prob - target)).astype(BF16)
 
-        @pl.loop(0, en)
+        @pl.loop(0, en, unroll=True)
         def _(i):
             sl = pl.ds(pl.multiple_of(i * estep, estep), estep)
             v = nn(sg[hs, :], tu[:, sl])
@@ -313,12 +313,12 @@
         hs = whole_half(h)
         finish(c_out[h])
 
-        @pl.loop(0, hn)
+        @pl.loop(0, hn, unroll=True)
         def _(i):
             sl = pl.ds(pl.multiple_of(i * hstep, hstep), hstep)
             ag[hs, sl] = (nt_dot(og[hs, :], wdf[sl, :]) * dgate[hs, sl]).astype(BF16)
 
-        @pl.loop(0, dn)
+        @pl.loop(0, dn, unroll=True)
         def _(i):
             sl = pl.ds(pl.multiple_of(i * dstep, dstep), dstep)
             v = nt_dot(ag[hs, :], wu[sl, :])

time: 89.2 us -> 85.4 us (0.957)
  Pallas kernels: 86.7 us -> 82.9 us
    pallas_call x1, Pallas kernels: 86.7 us -> 82.9 us  [local(): pl.pallas_call(functools.partial(kernel, nd, nt), out_shape=jax.ShapeDtyp...]
where the time goes in v3:
time: 85.4 us; the launch traced here: 85.2 us
  Pallas kernels  82.9 us (97%)
  local copies, waits for them, and re-layouts  1.67 us (2%)
    pallas_call x1, Pallas kernels, local(): pl.pallas_call(functools.partial(kernel, nd, nt), out_shape=jax.ShapeDtyp...  82.9 us

profile of v3, /device:TPU:0, one launch (start us, length us, event | category | flops | bytes accessed | tf_op | source)
XLA Modules:
  0.0 85.2 jit_solution(10399979819726813261)
XLA Ops:
  0.7 82.9 %shard_map.127 = f32[256,256]{1,0:T(8,128)} custom-call(bf16[256,256]{1,0:T(8,128)(2,1)} %resid.1, f32[1,1024]{1,0:T(1,128)} %bitcast.7, f32[1,1024]{1,0:T(1,128)} %bitcast.8, bf16[128,1024]{1,0:T(8,128)(2,1)} %up.1, f32[1,1024]{1,0:T(1,128)} %bitcast.9, bf16[1024,128]{1,0:T(8,128)(2,1)} %down.1, f32[1,1024]{1,0:T(1,128)} %bitcast.10, f32[1,256]{1,0:T(1,128)} %bitcast.11, ...), custom_call_target="tpu_custom_call" | custom-call | tf_op jit(solution)/shard_map/pallas_call | solution.py:420
  83.6 1.7 %copy.16 = f32[256,256]{1,0:T(8,128)} copy(f32[256,256]{1,0:T(8,128)} %shard_map.127) | data formatting | bytes 524288
